TPU v7x, 256 devices: a whole 4x4x8 slice. The times are simulated.
256 devices in a mesh: tm: 128 (over y_hi, z, x, core), mom: 2 (over y_lo).
Axes of the slice: x: 4, y: 4 (y_hi: 2, y_lo: 2; y = y_hi * 2 + y_lo), z: 8, core: 2. Of those that a mesh axis runs over, the one named last changes fastest.
Arguments:
- fields: bfloat16 [128, 4, 2, 512, 512], P('tm', 'mom'), may hold values from -1 to 1
- mom_pairs: int32 [6, 2], P('mom'), may hold values from 0 to 3, as said below
- deltas: int32 [4], replicated, may hold values from 0 to 3, each once
Outputs:
- time_traces: float32 [128, 2, 4, 6], P('tm', None, None, 'mom')
- summed_traces: float32 [2, 4, 6], P(None, None, 'mom')
Inputs may be any that keep to these rules, and one draw needn't show every extreme that they name: `mom_pairs`: column 0 may be any momentum; in row r, column 1 lies in momentum group r // 3, that is from (r // 3) * 2 to (r // 3) * 2 + 1.
All inputs are finite; a program needn't handle non-finite values.
Results may differ from a plain program's by a relative error of at most 0.0003.
Values may be sent and summed in bfloat16 or wider, within the bound.
No kernel may reach another device: no remote copies, remote signals or barrier semaphores. Data moves between devices by JAX's collectives and lax.ppermute only.
A program may use at most 128 MiB of HBM per device.

v0:
```python
import jax
import jax.numpy as jnp
from jax import lax
from jax.experimental import pallas as pl
from jax.experimental.pallas import tpu as pltpu
from jax.sharding import Mesh
from jax.sharding import PartitionSpec as P

TM = ("tm_0", "tm_1", "tm_2", "tm_3")
ALL = TM + ("mom",)
SIZES = (2, 8, 4, 2, 2)
F32 = jnp.float32
BF16 = jnp.bfloat16
N = 512
TIMES = 128
HALF = 64
ROWS = 384


def place(time):
    rest, core = divmod(time, 2)
    rest, x = divmod(rest, 4)
    half, z = divmod(rest, 8)
    return half, z, x, core


def time_of(half, z, x, core):
    return ((half * 8 + z) * 4 + x) * 2 + core


def device(time, group):
    return time * 2 + group


def each():
    return ((time, group) for time in range(TIMES) for group in range(2))


def earlier(time, group, distance):
    target = (time - distance) % TIMES
    crossed = place(target)[0] != place(time)[0]
    return target, group ^ crossed


def ring_route(distance):
    return [(device(t, g), device(*earlier(t, g, distance))) for t, g in each()]


def round_x_holder(time, group):
    half, z, x, core = place(time)
    if x == 1:
        target, kept = earlier(time, group, 4)
        half, z, _, _ = place(target)
        return time_of(half, z, 2, core), kept
    return time_of(half, z, (x + 1) % 4, core), group


def round_x_first():
    return [(device(t, g), device(*round_x_holder(t, g))) for t, g in each()]


def round_x_second():
    return [(device(*round_x_holder(t, g)), device(*earlier(t, g, 4))) for t, g in each()]


def partner_group_route():
    return [(device(t, g), device(t, 1 - g)) for t, g in each()]


def other_core_route():
    return [(device(t, g), device(t ^ 1, g)) for t, g in each()]


def to_core(core):
    return [(device(t ^ 1, g), device(t, g)) for t, g in each() if t % 2 == core]


def of_core(route, core):
    return [(a, b) for a, b in route if (a // 2) % 2 == core]


def moved(array, route):
    return lax.ppermute(array, ALL, route)


TIME, GROUP, PAIRS, OTHER_PAIRS, DELTAS = 0, 1, 2, 8, 14
SMEM = pl.BlockSpec(memory_space=pltpu.SMEM)
VMEM = pl.BlockSpec(memory_space=pltpu.VMEM)
ANYWHERE = pl.BlockSpec(memory_space=pl.ANY)
HBM = pl.BlockSpec(memory_space=pltpu.HBM)


def fold(block):
    rows, columns = block.shape
    block = block.reshape(rows // 8, 8, columns).sum(0)
    return sum(block[:, i * 128 : (i + 1) * 128] for i in range(columns // 128))


def diagonal(block):
    rows = lax.broadcasted_iota(jnp.int32, block.shape, 0)
    columns = lax.broadcasted_iota(jnp.int32, block.shape, 1)
    return jnp.where(rows == columns, block, 0.0)


def product_terms(source, target, diff, total):
    direct = jnp.zeros((8, 128), F32)

    def dot(left, right):
        return jnp.dot(left, right, preferred_element_type=F32)

    for tile in range(2):
        columns = slice(tile * 256, (tile + 1) * 256)
        right_re = jnp.concatenate([piece[0, :, columns] for piece in target], axis=0)
        right_im = jnp.concatenate([piece[1, :, columns] for piece in target], axis=0)
        for half in range(2):
            rows = slice(half * 256, (half + 1) * 256)
            left_re, left_im = source[0, rows], source[1, rows]
            q_re = dot(left_re, right_re) - dot(left_im, right_im)
            q_im = dot(left_re, right_im) + dot(left_im, right_re)
            if half == tile:
                for k in range(2):
                    at = slice(k * 128, (k + 1) * 128)
                    direct = direct + fold(diagonal(q_re[at, at]))
            diff[rows, columns] = q_re - q_im
            total[rows, columns] = q_re + q_im
    box = jnp.zeros((8, 128), F32)
    for i in range(4):
        rows = slice(i * 128, (i + 1) * 128)
        for j in range(4):
            columns = slice(j * 128, (j + 1) * 128)
            box = box + fold(diff[rows, columns] * total[columns, rows].T)
    return direct, box


def add_terms(table, fields, result, sep, pieces, diff, total):
    time, group = table[TIME], table[GROUP]
    crossed = (time % HALF) + sep >= HALF
    shown = jnp.where(crossed, 1 - group, group)
    at = jnp.where(crossed, OTHER_PAIRS, PAIRS)
    row = sum(jnp.where(table[DELTAS + i] == sep - 1, i, 0) for i in range(4))
    lanes = lax.broadcasted_iota(jnp.int32, (1, 128), 1)
    for k in range(3):
        source = table[at + 2 * k]
        slot = source % 2 + jnp.where(source // 2 == group, 0, 2)
        momentum = table[at + 2 * k + 1] - 2 * shown

        target = [piece.at[momentum] for piece in pieces]
        direct, box = product_terms(fields.at[slot], target, diff.at[k % 2], total.at[k % 2])
        result = jnp.where(lanes == k * 4 + row, jnp.sum(direct), result)
        result = jnp.where(lanes == 12 + k * 4 + row, jnp.sum(box), result)
    return result


def first_body(
    table_in, own, other, near, two, out, fields, table, near_in, two_in, diff, total, sems
):
    moves = [
        (table_in, table),
        (own, fields.at[0:2]),
        (other, fields.at[2:4]),
        (near, near_in),
        (two, two_in),
    ]
    copies = [pltpu.make_async_copy(a, b, sems.at[i]) for i, (a, b) in enumerate(moves)]
    for copy in copies[:3]:
        copy.start()
    copies[0].wait()
    core = table[TIME] % 2
    pl.when(core == 0)(copies[3].start)
    copies[4].start()
    copies[1].wait()
    copies[2].wait()
    out[...] = jnp.zeros((1, 128), F32)

    @pl.when(core == 0)
    def _():
        copies[3].wait()
        out[...] = add_terms(table, fields, out[...], 1, [near_in], diff, total)

    copies[4].wait()
    out[...] = add_terms(table, fields, out[...], 2, [two_in], diff, total)


def swapped_body(table, fields, later, before, out, diff, total):
    sep = jnp.where(table[TIME] % 2 == 0, 3, 1)
    out[...] = add_terms(table, fields, before[...], sep, [later], diff, total)


def late_body(table, fields, later, before, out, diff, total):
    out[...] = before[...]

    @pl.when(table[TIME] % 2 == 1)
    def _():
        out[...] = add_terms(table, fields, before[...], 3, [later], diff, total)


def four_body(table, fields, around, onward, rest, before, out, around_in, diff, total, sems):
    core = table[TIME] % 2

    def put(*later):
        result = add_terms(table, fields, before[...], 4, later, diff, total)
        out[...] = jnp.broadcast_to(result[None], out.shape)

    @pl.when(core == 0)
    def _():
        copy = pltpu.make_async_copy(around, around_in, sems.at[0])
        copy.start()
        copy.wait()
        put(around_in)

    @pl.when(core == 1)
    def _():
        put(onward, rest)


ROW = jax.ShapeDtypeStruct((1, 128), F32)
FIELDS = jax.ShapeDtypeStruct((4, 2, N, N), BF16)
PLANES = pltpu.VMEM((2, 2, N, N), BF16)
WORK = [pltpu.VMEM((2, N, N), F32), pltpu.VMEM((2, N, N), F32)]


def stage(body, operands, spaces, outs, scratch, products):
    call = pl.pallas_call(
        body,
        in_specs=spaces,
        out_specs=jax.tree.map(lambda _: VMEM, outs),
        out_shape=outs,
        scratch_shapes=scratch,
        compiler_params=pltpu.CompilerParams(vmem_limit_bytes=20 << 20),
        cost_estimate=pl.CostEstimate(
            flops=products * 8 * N**3, bytes_accessed=5 << 20, transcendentals=0
        ),
    )
    return call(*operands)


def zero_body(table, out):
    out[...] = jnp.zeros((1, 128), F32)


def mark_body(before, _, out):
    out[...] = before[...]


def finish_body(table, gathered, _, time_out, sum_out, time_row, sum_row, sems):
    time, group = table[TIME], table[GROUP]
    lanes = lax.broadcasted_iota(jnp.int32, (1, 128), 1)
    sep = jnp.zeros((1, 128), jnp.int32)
    for r in range(4):
        sep = jnp.where(lanes % 4 == r, table[DELTAS + r] + 1, sep)

    def value(at):
        crossed = (at % HALF) + sep >= HALF
        return jnp.where(crossed, gathered[2 * at + 1 - group], gathered[2 * at + group])

    def spread(row, out):
        for val in range(2):
            for k in range(3):
                at = val * 12 + k * 4
                shifted = pltpu.roll(row, 128 - at, 1) if at else row
                out[k, val : val + 1, :] = shifted[:, 0:4]

    spread(value(time), time_row.at[0])
    mine = pltpu.make_async_copy(time_row, time_out, sems.at[0])
    mine.start()
    total = jnp.zeros((1, 128), F32)
    for at in range(TIMES):
        if at % HALF < HALF - 4:
            total = total + gathered[2 * at + group]
        else:
            total = total + value(at)
    spread(total, sum_row)
    both = pltpu.make_async_copy(sum_row, sum_out, sems.at[1])
    both.start()
    mine.wait()
    both.wait()


def finished(table, gathered, ready):
    shapes = ((1, 3, 2, 4), (3, 2, 4))
    call = pl.pallas_call(
        finish_body,
        in_specs=[SMEM, VMEM, ANYWHERE],
        out_specs=(HBM, HBM),
        out_shape=tuple(jax.ShapeDtypeStruct(shape, F32) for shape in shapes),
        scratch_shapes=[pltpu.VMEM(shape, F32) for shape in shapes]
        + [pltpu.SemaphoreType.DMA((2,))],
        name="finish",
    )
    time_traces, summed_traces = call(table, gathered, ready)
    return time_traces.transpose(0, 2, 3, 1), summed_traces.transpose(1, 2, 0)


def per_device(fields, mom_pairs, deltas):
    own = fields[0]
    time = lax.axis_index(TM).astype(jnp.int32)
    group = lax.axis_index("mom").astype(jnp.int32)

    two = moved(own, ring_route(2))
    other_pairs = moved(mom_pairs, partner_group_route())
    other = moved(own, partner_group_route())
    around = moved(own, of_core(round_x_first(), 0))
    near = moved(own, to_core(0))
    table = jnp.concatenate(
        [jnp.stack([time, group]), mom_pairs.reshape(-1), other_pairs.reshape(-1), deltas]
    )
    zero = pl.pallas_call(zero_body, in_specs=[SMEM], out_specs=VMEM, out_shape=ROW, name="zero")
    mark = pl.pallas_call(
        mark_body, in_specs=[VMEM, VMEM], out_specs=VMEM, out_shape=ROW, name="mark"
    )
    ready = mark(zero(table), own)
    around = moved(around, of_core(round_x_second(), 0))
    swap = moved(two, other_core_route())
    onward = moved(two[:, :, :ROWS], of_core(ring_route(2), 1))
    rest = moved(own[:, :, ROWS:], of_core(round_x_first(), 1))
    rest = moved(rest, of_core(round_x_second(), 1))

    result, all_fields = stage(
        first_body,
        (table, own, other, near, two),
        [HBM, VMEM] + [ANYWHERE] * 3,
        (ROW, FIELDS),
        [pltpu.SMEM((18,), jnp.int32), PLANES, PLANES] + WORK + [pltpu.SemaphoreType.DMA((5,))],
        6,
    )
    late = moved(around, to_core(1))
    result = stage(
        swapped_body, (table, all_fields, swap, result), [SMEM] + [VMEM] * 3, ROW, WORK, 3
    )
    result = stage(late_body, (table, all_fields, late, result), [SMEM] + [VMEM] * 3, ROW, WORK, 3)
    rows = stage(
        four_body,
        (table, all_fields, around, onward, rest, result),
        [SMEM, VMEM, ANYWHERE, VMEM, VMEM, VMEM],
        jax.ShapeDtypeStruct((2 * TIMES, 1, 128), F32),
        [PLANES] + WORK + [pltpu.SemaphoreType.DMA((1,))],
        3,
    )
    gathered = lax.all_to_all(rows, ALL, 0, 0, tiled=True)
    return finished(table, gathered, ready)


def solution(mesh):
    finer = Mesh(mesh.devices.reshape(SIZES), ALL)
    in_specs = (P(TM, "mom", None, None, None), P("mom", None), P())
    out_specs = (P(TM, None, None, "mom"), P(None, None, "mom"))
    return jax.shard_map(
        per_device, mesh=finer, in_specs=in_specs, out_specs=out_specs, check_vma=False
    )
```

profile of v0, /device:TPU:1, one launch (start us, length us, event | category | flops | bytes accessed | tf_op | source)
XLA Modules:
  0.0 134.7 jit_solution(6003338368040660221)
XLA Ops:
  0.6 0.0 copy-start
  0.7 0.9 collective-permute-start.4
  1.6 11.1 %collective-permute-start.3 = (bf16[2,2,512,512]{3,2,1,0:T(8,128)(2,1)}, bf16[2,2,512,512]{3,2,1,0:T(8,128)(2,1)}, u32[]{:S(2)}, u32[]{:S(2)}) collective-permute-start(bf16[2,2,512,512]{3,2,1,0:T(8,128)(2,1)} %bitcast.6), channel_id=1, source_target_pairs={{0,253},{1,252},{2,255},{3,254},{4,0},{5,1},{6,2},{7,3},{8,4},{9,5... | collective-permute-start | bytes 6291464 | tf_op jit(solution)/shard_map/ppermute | solution.py:83
  12.7 2.0 %collective-permute-start.5 = (bf16[2,2,512,512]{3,2,1,0:T(8,128)(2,1)S(1)}, bf16[2,2,512,512]{3,2,1,0:T(8,128)(2,1)}, u32[]{:S(2)}, u32[]{:S(2)}) collective-permute-start(bf16[2,2,512,512]{3,2,1,0:T(8,128)(2,1)S(1)} %collective-permute-done.4), channel_id=1, source_target_pairs={{4,249},{5,248},{249,253},{248,252},{12,0},{13,1},{0,4},{1,5},{20,... | collective-permute-start | bytes 6291464 | tf_op jit(solution)/shard_map/ppermute | solution.py:83
  14.7 29.4 %collective-permute-start.2 = (bf16[2,2,512,512]{3,2,1,0:T(8,128)(2,1)}, bf16[2,2,512,512]{3,2,1,0:T(8,128)(2,1)}, u32[]{:S(2)}, u32[]{:S(2)}) collective-permute-start(bf16[2,2,512,512]{3,2,1,0:T(8,128)(2,1)} %bitcast.8), channel_id=1, source_target_pairs={{2,0},{3,1},{6,4},{7,5},{10,8},{11,9},{14,12},{15,13},{18,16},{19,... | collective-permute-start | bytes 6291464 | tf_op jit(solution)/shard_map/ppermute | solution.py:83
  44.2 11.6 %collective-permute-done.3.two = bf16[2,2,512,512]{3,2,1,0:T(8,128)(2,1)} collective-permute-done((bf16[2,2,512,512]{3,2,1,0:T(8,128)(2,1)}, bf16[2,2,512,512]{3,2,1,0:T(8,128)(2,1)}, u32[]{:S(2)}, u32[]{:S(2)}) %collective-permute-start.3) | collective-permute-done | bytes 2097184 | tf_op jit(solution)/shard_map/ppermute | solution.py:83
  55.7 3.1 %collective-permute-start.10 = (bf16[2,2,512,512]{3,2,1,0:T(8,128)(2,1)}, bf16[2,2,512,512]{3,2,1,0:T(8,128)(2,1)}, u32[]{:S(2)}, u32[]{:S(2)}) collective-permute-start(bf16[2,2,512,512]{3,2,1,0:T(8,128)(2,1)} %collective-permute-done.3.two), channel_id=1, source_target_pairs={{0,2},{1,3},{2,0},{3,1},{4,6},{5,7},{6,4},{7,5},{8,10},{9,11},{10,... | collective-permute-start | bytes 6291464 | tf_op jit(solution)/shard_map/ppermute | solution.py:83
  58.9 1.3 collective-permute-start.9
  60.2 0.1 collective-permute-start
  60.3 1.1 slice.9
  61.4 1.9 %collective-permute-done = s32[3,2]{0,1:T(2,128)S(1)} collective-permute-done((s32[3,2]{0,1:T(2,128)}, s32[3,2]{0,1:T(2,128)S(1)}, u32[]{:S(2)}, u32[]{:S(2)}) %collective-permute-start) | collective-permute-done | bytes 56 | tf_op jit(solution)/shard_map/ppermute | solution.py:83
  63.3 1.9 %collective-permute-start.7 = (bf16[2,2,128,512]{3,2,1,0:T(8,128)(2,1)S(1)}, bf16[2,2,128,512]{3,2,1,0:T(8,128)(2,1)S(1)}, u32[]{:S(2)}, u32[]{:S(2)}) collective-permute-start(bf16[2,2,128,512]{3,2,1,0:T(8,128)(2,1)S(1)} %slice.9), channel_id=1, source_target_pairs={{2,6},{3,7},{6,251},{7,250},{10,14},{11,15},{14,2},{15,3},{18,22},... | collective-permute-start | bytes 1572872 | tf_op jit(solution)/shard_map/ppermute | solution.py:83
  65.2 2.7 %slice.8 = bf16[2,2,384,512]{3,2,1,0:T(8,128)(2,1)} slice(bf16[2,2,512,512]{3,2,1,0:T(8,128)(2,1)} %collective-permute-done.3.two), slice={[0:2], [0:2], [0:384], [0:512]} | slice | bytes 3145728 | tf_op jit(solution)/shard_map/slice | solution.py:314
  67.9 6.5 %collective-permute-done.7 = bf16[2,2,128,512]{3,2,1,0:T(8,128)(2,1)S(1)} collective-permute-done((bf16[2,2,128,512]{3,2,1,0:T(8,128)(2,1)S(1)}, bf16[2,2,128,512]{3,2,1,0:T(8,128)(2,1)S(1)}, u32[]{:S(2)}, u32[]{:S(2)}) %collective-permute-start.7) | collective-permute-done | bytes 524320 | tf_op jit(solution)/shard_map/ppermute | solution.py:83
  74.4 8.3 %collective-permute-start.6 = (bf16[2,2,384,512]{3,2,1,0:T(8,128)(2,1)}, bf16[2,2,384,512]{3,2,1,0:T(8,128)(2,1)}, u32[]{:S(2)}, u32[]{:S(2)}) collective-permute-start(bf16[2,2,384,512]{3,2,1,0:T(8,128)(2,1)} %slice.8), channel_id=1, source_target_pairs={{2,255},{3,254},{6,2},{7,3},{10,6},{11,7},{14,10},{15,11},{18,14},... | collective-permute-start | bytes 4718600 | tf_op jit(solution)/shard_map/ppermute | solution.py:83
  82.8 0.1 copy.7
  82.8 0.1 reshape.10
  82.9 0.1 copy.8
  83.0 0.1 reshape.11
  83.1 0.1 concatenate.3.table_in.table
  83.2 0.0 collective-permute-done.1.other
  83.2 1.9 %collective-permute-start.8 = (bf16[2,2,128,512]{3,2,1,0:T(8,128)(2,1)S(1)}, bf16[2,2,128,512]{3,2,1,0:T(8,128)(2,1)S(1)}, u32[]{:S(2)}, u32[]{:S(2)}) collective-permute-start(bf16[2,2,128,512]{3,2,1,0:T(8,128)(2,1)S(1)} %collective-permute-done.7), channel_id=1, source_target_pairs={{6,251},{7,250},{251,255},{250,254},{14,2},{15,3},{2,6},{3,7},{22,... | collective-permute-start | bytes 1572872 | tf_op jit(solution)/shard_map/ppermute | solution.py:83
  85.1 6.2 %shard_map.50 = (f32[1,128]{1,0:T(1,128)S(1)}, bf16[4,2,512,512]{3,2,1,0:T(8,128)(2,1)S(1)}) custom-call(s32[18]{0:T(128)S(1)} %concatenate.3.table_in.table, bf16[2,2,512,512]{3,2,1,0:T(8,128)(2,1)S(1)} %bitcast.11, bf16[2,2,512,512]{3,2,1,0:T(8,128)(2,1)} %collective-permute-done.1.other, bf16[2,2,512,512]{3,2,1,0:T(8,128)(2,1)} %collective-permute-done.2.near, ...), custom_call_target="tpu_custom_call" | custom-call | flops 6442450944 | bytes 5242880 | tf_op jit(solution)/shard_map/pallas_call | solution.py:234
  91.3 5.3 %shard_map.51.before = f32[1,128]{1,0:T(1,128)S(1)} custom-call(s32[18]{0:T(128)S(1)} %concatenate.3.table_in.table, bf16[4,2,512,512]{3,2,1,0:T(8,128)(2,1)S(1)} %get-tuple-element.6.fields, bf16[2,2,512,512]{3,2,1,0:T(8,128)(2,1)} %collective-permute-done.10.later, f32[1,128]{1,0:T(1,128)S(1)} %get-tuple-element.7.before), custom_call_target="tpu_custom_call" | custom-call | flops 3221225472 | bytes 5242880 | tf_op jit(solution)/shard_map/pallas_call | solution.py:234
  96.6 5.3 %shard_map.52.before = f32[1,128]{1,0:T(1,128)S(1)} custom-call(s32[18]{0:T(128)S(1)} %concatenate.3.table_in.table, bf16[4,2,512,512]{3,2,1,0:T(8,128)(2,1)S(1)} %get-tuple-element.6.fields, bf16[2,2,512,512]{3,2,1,0:T(8,128)(2,1)} %collective-permute-done.9.later, f32[1,128]{1,0:T(1,128)S(1)} %shard_map.51.before), custom_call_target="tpu_custom_call" | custom-call | flops 3221225472 | bytes 5242880 | tf_op jit(solution)/shard_map/pallas_call | solution.py:234
  102.0 6.1 %shard_map.53 = f32[256,1,128]{2,1,0:T(1,128)} custom-call(s32[18]{0:T(128)S(1)} %concatenate.3.table_in.table, bf16[4,2,512,512]{3,2,1,0:T(8,128)(2,1)S(1)} %get-tuple-element.6.fields, bf16[2,2,512,512]{3,2,1,0:T(8,128)(2,1)} %collective-permute-done.5.around, bf16[2,2,384,512]{3,2,1,0:T(8,128)(2,1)} %collective-permute-done.6.onward, ...), custom_call_target="tpu_custom_call" | custom-call | flops 3221225472 | bytes 5242880 | tf_op jit(solution)/shard_map/pallas_call | solution.py:234
  108.0 11.3 %all-to-all-start = ((f32[256,1,128]{2,1,0:T(1,128)}), f32[256,1,128]{2,1,0:T(1,128)S(1)}, u32[]{:S(2)}, u32[]{:S(2)}) async-start(f32[256,1,128]{2,1,0:T(1,128)} %shard_map.53), calls=%async_computation | async-start | bytes 262144 | tf_op jit(solution)/shard_map/all_to_all | solution.py:339
  119.3 1.2 zero.1.before
  120.5 2.2 %mark.1._ = f32[1,128]{1,0:T(1,128)} custom-call(f32[1,128]{1,0:T(1,128)} %zero.1.before, bf16[2,2,512,512]{3,2,1,0:T(8,128)(2,1)} %bitcast.10), custom_call_target="tpu_custom_call" | custom-call | tf_op jit(solution)/shard_map/mark/pallas_call | solution.py:311
  122.7 9.5 %all-to-all-done.gathered = f32[256,1,128]{2,1,0:T(1,128)S(1)} async-done(((f32[256,1,128]{2,1,0:T(1,128)}), f32[256,1,128]{2,1,0:T(1,128)S(1)}, u32[]{:S(2)}, u32[]{:S(2)}) %all-to-all-start) | async-done | bytes 131104 | tf_op jit(solution)/shard_map/all_to_all | solution.py:339
  132.2 0.7 copy-done.2
  132.8 1.7 %finish.1 = (f32[1,3,2,4]{3,2,1,0:T(2,128)}, f32[3,2,4]{2,1,0:T(2,128)}) custom-call(s32[18]{0:T(128)} %copy-done.1, f32[256,1,128]{2,1,0:T(1,128)} %copy-done.2, f32[1,128]{1,0:T(1,128)} %mark.1._), custom_call_target="tpu_custom_call" | custom-call | tf_op jit(solution)/shard_map/finish/pallas_call | solution.py:290
  (16 shorter events, 0.0 us)
Async XLA Ops:
  0.6 82.1 %copy-start.3 = (s32[3,2]{0,1:T(2,128)S(1)}, s32[3,2]{0,1:T(2,128)}, u32[]{:S(2)}) copy-start(s32[3,2]{0,1:T(2,128)} %param.4) | copy-start | bytes 76
  0.6 82.5 %copy-start.4 = (s32[4]{0:T(128)S(1)}, s32[4]{0:T(128)}, u32[]{:S(2)}) copy-start(s32[4]{0:T(128)} %param.5) | copy-start | bytes 52
  0.6 84.5 %copy-start = (bf16[1,2,2,512,512]{4,3,2,1,0:T(8,128)(2,1)S(1)}, bf16[1,2,2,512,512]{4,3,2,1,0:T(8,128)(2,1)}, u32[]{:S(2)}) copy-start(bf16[1,2,2,512,512]{4,3,2,1,0:T(8,128)(2,1)} %param.3) | copy-start | bytes 6291460
  0.7 12.1 %collective-permute-start.4 = (bf16[2,2,512,512]{3,2,1,0:T(8,128)(2,1)}, bf16[2,2,512,512]{3,2,1,0:T(8,128)(2,1)S(1)}, u32[]{:S(2)}, u32[]{:S(2)}) collective-permute-start(bf16[2,2,512,512]{3,2,1,0:T(8,128)(2,1)} %bitcast.5), channel_id=1, source_target_pairs={{0,4},{1,5},{4,249},{5,248},{8,12},{9,13},{12,0},{13,1},{16,20},{1... | collective-permute-start | bytes 6291464 | tf_op jit(solution)/shard_map/ppermute | solution.py:83
  1.6 54.1 %collective-permute-start.3 = (bf16[2,2,512,512]{3,2,1,0:T(8,128)(2,1)}, bf16[2,2,512,512]{3,2,1,0:T(8,128)(2,1)}, u32[]{:S(2)}, u32[]{:S(2)}) collective-permute-start(bf16[2,2,512,512]{3,2,1,0:T(8,128)(2,1)} %bitcast.6), channel_id=1, source_target_pairs={{0,253},{1,252},{2,255},{3,254},{4,0},{5,1},{6,2},{7,3},{8,4},{9,5... | collective-permute-start | bytes 6291464 | tf_op jit(solution)/shard_map/ppermute | solution.py:83
  12.7 46.2 %collective-permute-start.5 = (bf16[2,2,512,512]{3,2,1,0:T(8,128)(2,1)S(1)}, bf16[2,2,512,512]{3,2,1,0:T(8,128)(2,1)}, u32[]{:S(2)}, u32[]{:S(2)}) collective-permute-start(bf16[2,2,512,512]{3,2,1,0:T(8,128)(2,1)S(1)} %collective-permute-done.4), channel_id=1, source_target_pairs={{4,249},{5,248},{249,253},{248,252},{12,0},{13,1},{0,4},{1,5},{20,... | collective-permute-start | bytes 6291464 | tf_op jit(solution)/shard_map/ppermute | solution.py:83
  14.7 68.5 %collective-permute-start.1 = (bf16[2,2,512,512]{3,2,1,0:T(8,128)(2,1)}, bf16[2,2,512,512]{3,2,1,0:T(8,128)(2,1)}, u32[]{:S(2)}, u32[]{:S(2)}) collective-permute-start(bf16[2,2,512,512]{3,2,1,0:T(8,128)(2,1)} %bitcast.7), channel_id=1, source_target_pairs={{0,1},{1,0},{2,3},{3,2},{4,5},{5,4},{6,7},{7,6},{8,9},{9,8},{10,11... | collective-permute-start | bytes 6291464 | tf_op jit(solution)/shard_map/ppermute | solution.py:83
  14.7 70.4 %collective-permute-start.2 = (bf16[2,2,512,512]{3,2,1,0:T(8,128)(2,1)}, bf16[2,2,512,512]{3,2,1,0:T(8,128)(2,1)}, u32[]{:S(2)}, u32[]{:S(2)}) collective-permute-start(bf16[2,2,512,512]{3,2,1,0:T(8,128)(2,1)} %bitcast.8), channel_id=1, source_target_pairs={{2,0},{3,1},{6,4},{7,5},{10,8},{11,9},{14,12},{15,13},{18,16},{19,... | collective-permute-start | bytes 6291464 | tf_op jit(solution)/shard_map/ppermute | solution.py:83
  55.7 35.6 %collective-permute-start.10 = (bf16[2,2,512,512]{3,2,1,0:T(8,128)(2,1)}, bf16[2,2,512,512]{3,2,1,0:T(8,128)(2,1)}, u32[]{:S(2)}, u32[]{:S(2)}) collective-permute-start(bf16[2,2,512,512]{3,2,1,0:T(8,128)(2,1)} %collective-permute-done.3.two), channel_id=1, source_target_pairs={{0,2},{1,3},{2,0},{3,1},{4,6},{5,7},{6,4},{7,5},{8,10},{9,11},{10,... | collective-permute-start | bytes 6291464 | tf_op jit(solution)/shard_map/ppermute | solution.py:83
  58.9 37.8 %collective-permute-start.9 = (bf16[2,2,512,512]{3,2,1,0:T(8,128)(2,1)}, bf16[2,2,512,512]{3,2,1,0:T(8,128)(2,1)}, u32[]{:S(2)}, u32[]{:S(2)}) collective-permute-start(bf16[2,2,512,512]{3,2,1,0:T(8,128)(2,1)} %collective-permute-done.5.around), channel_id=1, source_target_pairs={{0,2},{1,3},{4,6},{5,7},{8,10},{9,11},{12,14},{13,15},{16,18},{17,... | collective-permute-start | bytes 6291464 | tf_op jit(solution)/shard_map/ppermute | solution.py:83
  60.2 3.1 %collective-permute-start = (s32[3,2]{0,1:T(2,128)}, s32[3,2]{0,1:T(2,128)S(1)}, u32[]{:S(2)}, u32[]{:S(2)}) collective-permute-start(s32[3,2]{0,1:T(2,128)} %param.4), channel_id=1, source_target_pairs={{0,1},{1,0},{2,3},{3,2},{4,5},{5,4},{6,7},{7,6},{8,9},{9,8},{10,11... | collective-permute-start | bytes 80 | tf_op jit(solution)/shard_map/ppermute | solution.py:83
  63.3 11.1 %collective-permute-start.7 = (bf16[2,2,128,512]{3,2,1,0:T(8,128)(2,1)S(1)}, bf16[2,2,128,512]{3,2,1,0:T(8,128)(2,1)S(1)}, u32[]{:S(2)}, u32[]{:S(2)}) collective-permute-start(bf16[2,2,128,512]{3,2,1,0:T(8,128)(2,1)S(1)} %slice.9), channel_id=1, source_target_pairs={{2,6},{3,7},{6,251},{7,250},{10,14},{11,15},{14,2},{15,3},{18,22},... | collective-permute-start | bytes 1572872 | tf_op jit(solution)/shard_map/ppermute | solution.py:83
  74.4 27.5 %collective-permute-start.6 = (bf16[2,2,384,512]{3,2,1,0:T(8,128)(2,1)}, bf16[2,2,384,512]{3,2,1,0:T(8,128)(2,1)}, u32[]{:S(2)}, u32[]{:S(2)}) collective-permute-start(bf16[2,2,384,512]{3,2,1,0:T(8,128)(2,1)} %slice.8), channel_id=1, source_target_pairs={{2,255},{3,254},{6,2},{7,3},{10,6},{11,7},{14,10},{15,11},{18,14},... | collective-permute-start | bytes 4718600 | tf_op jit(solution)/shard_map/ppermute | solution.py:83
  83.2 18.8 %copy-start.1 = (s32[18]{0:T(128)}, s32[18]{0:T(128)S(1)}, u32[]{:S(2)}) copy-start(s32[18]{0:T(128)S(1)} %concatenate.3.table_in.table) | copy-start | bytes 220
  83.2 18.8 %collective-permute-start.8 = (bf16[2,2,128,512]{3,2,1,0:T(8,128)(2,1)S(1)}, bf16[2,2,128,512]{3,2,1,0:T(8,128)(2,1)S(1)}, u32[]{:S(2)}, u32[]{:S(2)}) collective-permute-start(bf16[2,2,128,512]{3,2,1,0:T(8,128)(2,1)S(1)} %collective-permute-done.7), channel_id=1, source_target_pairs={{6,251},{7,250},{251,255},{250,254},{14,2},{15,3},{2,6},{3,7},{22,... | collective-permute-start | bytes 1572872 | tf_op jit(solution)/shard_map/ppermute | solution.py:83
  108.0 24.1 %all-to-all-start = ((f32[256,1,128]{2,1,0:T(1,128)}), f32[256,1,128]{2,1,0:T(1,128)S(1)}, u32[]{:S(2)}, u32[]{:S(2)}) async-start(f32[256,1,128]{2,1,0:T(1,128)} %shard_map.53), calls=%async_computation | async-start | bytes 262144 | tf_op jit(solution)/shard_map/all_to_all | solution.py:339
  132.2 0.7 copy-start.2
where the time goes:
time: 135 us
  starting transfers between devices  71.4 us (53%)
  waiting for transfers between devices  29.6 us (22%)
  Pallas kernels  27.9 us (21%)
  local copies, waits for them, and re-layouts  4.85 us (4%)
    ppermute x11, starting transfers between devices, moved(): return lax.ppermute(array, ALL, route)  60.1 us
    pallas_call x4, Pallas kernels, stage(): return call(*operands)  22.8 us
    ppermute x11, waiting for transfers between devices, moved(): return lax.ppermute(array, ALL, route)  20.1 us
    all_to_all x1, starting transfers between devices, per_device(): gathered = lax.all_to_all(rows, ALL, 0, 0, tiled=True)  11.3 us
    all_to_all x1, waiting for transfers between devices, per_device(): gathered = lax.all_to_all(rows, ALL, 0, 0, tiled=True)  9.51 us
    pallas_call x2, Pallas kernels, per_device(): ready = mark(zero(table), own)  3.35 us
  transfers between devices with their start and end apart: 12, of which 4 were waited for; matrix products, arithmetic and copies ran while one was open for 3% of the time, Pallas kernels for 15%

commit v1 on v0

--- a/solution.py
+++ b/solution.py
@@ -1,3 +1,5 @@
+import functools
+
 import jax
 import jax.numpy as jnp
 from jax import lax
@@ -14,7 +16,7 @@
 N = 512
 TIMES = 128
 HALF = 64
-ROWS = 384
+ROWS = 416
 
 
 def place(time):
@@ -65,10 +67,6 @@
 
 def partner_group_route():
     return [(device(t, g), device(t, 1 - g)) for t, g in each()]
-
-
-def other_core_route():
-    return [(device(t, g), device(t ^ 1, g)) for t, g in each()]
 
 
 def to_core(core):
@@ -151,23 +149,14 @@
     return result
 
 
-def first_body(
-    table_in, own, other, near, two, out, fields, table, near_in, two_in, diff, total, sems
-):
-    moves = [
-        (table_in, table),
-        (own, fields.at[0:2]),
-        (other, fields.at[2:4]),
-        (near, near_in),
-        (two, two_in),
-    ]
+def first_body(table_in, own, other, near, out, fields, table, near_in, diff, total, sems):
+    moves = [(table_in, table), (own, fields.at[0:2]), (other, fields.at[2:4]), (near, near_in)]
     copies = [pltpu.make_async_copy(a, b, sems.at[i]) for i, (a, b) in enumerate(moves)]
     for copy in copies[:3]:
         copy.start()
     copies[0].wait()
     core = table[TIME] % 2
     pl.when(core == 0)(copies[3].start)
-    copies[4].start()
     copies[1].wait()
     copies[2].wait()
     out[...] = jnp.zeros((1, 128), F32)
@@ -177,13 +166,15 @@
         copies[3].wait()
         out[...] = add_terms(table, fields, out[...], 1, [near_in], diff, total)
 
-    copies[4].wait()
-    out[...] = add_terms(table, fields, out[...], 2, [two_in], diff, total)
-
-
-def swapped_body(table, fields, later, before, out, diff, total):
-    sep = jnp.where(table[TIME] % 2 == 0, 3, 1)
-    out[...] = add_terms(table, fields, before[...], sep, [later], diff, total)
+
+def by_core_body(table, fields, later0, later1, before, out, diff, total, *, seps):
+    for core, later in enumerate((later0, later1)):
+
+        @pl.when(table[TIME] % 2 == core)
+        def _(core=core, later=later):
+            out[...] = add_terms(
+                table, fields, before[...], seps[core], [later], diff, total
+            )
 
 
 def late_body(table, fields, later, before, out, diff, total):
@@ -296,7 +287,7 @@
     time = lax.axis_index(TM).astype(jnp.int32)
     group = lax.axis_index("mom").astype(jnp.int32)
 
-    two = moved(own, ring_route(2))
+    two1 = moved(own, of_core(ring_route(2), 1))
     other_pairs = moved(mom_pairs, partner_group_route())
     other = moved(own, partner_group_route())
     around = moved(own, of_core(round_x_first(), 0))
@@ -310,22 +301,37 @@
     )
     ready = mark(zero(table), own)
     around = moved(around, of_core(round_x_second(), 0))
-    swap = moved(two, other_core_route())
-    onward = moved(two[:, :, :ROWS], of_core(ring_route(2), 1))
+    two0 = moved(own, of_core(ring_route(2), 0))
+    onward = moved(two1[:, :, :ROWS], of_core(ring_route(2), 1))
+    swap1 = moved(two1, to_core(0))
+    swap0 = moved(two0, to_core(1))
     rest = moved(own[:, :, ROWS:], of_core(round_x_first(), 1))
     rest = moved(rest, of_core(round_x_second(), 1))
 
     result, all_fields = stage(
         first_body,
-        (table, own, other, near, two),
-        [HBM, VMEM] + [ANYWHERE] * 3,
+        (table, own, other, near),
+        [HBM, VMEM] + [ANYWHERE] * 2,
         (ROW, FIELDS),
-        [pltpu.SMEM((18,), jnp.int32), PLANES, PLANES] + WORK + [pltpu.SemaphoreType.DMA((5,))],
-        6,
+        [pltpu.SMEM((18,), jnp.int32), PLANES] + WORK + [pltpu.SemaphoreType.DMA((4,))],
+        3,
+    )
+    result = stage(
+        functools.partial(by_core_body, seps=(2, 2)),
+        (table, all_fields, two0, two1, result),
+        [SMEM] + [VMEM] * 4,
+        ROW,
+        WORK,
+        3,
     )
     late = moved(around, to_core(1))
     result = stage(
-        swapped_body, (table, all_fields, swap, result), [SMEM] + [VMEM] * 3, ROW, WORK, 3
+        functools.partial(by_core_body, seps=(3, 1)),
+        (table, all_fields, swap1, swap0, result),
+        [SMEM] + [VMEM] * 4,
+        ROW,
+        WORK,
+        3,
     )
     result = stage(late_body, (table, all_fields, late, result), [SMEM] + [VMEM] * 3, ROW, WORK, 3)
     rows = stage(

time: 135 us -> 141 us (1.044)
  waiting for transfers between devices: 29.6 us -> 44.9 us
  starting transfers between devices: 71.4 us -> 57.1 us
  local copies, waits for them, and re-layouts: 4.85 us -> 7.79 us
    ppermute x11 -> x13, waiting for transfers between devices: 20.1 us -> 35.5 us  [moved(): return lax.ppermute(array, ALL, route)]
    ppermute x11 -> x13, starting transfers between devices: 60.1 us -> 49.2 us  [moved(): return lax.ppermute(array, ALL, route)]
    all_to_all x1, starting transfers between devices: 11.3 us -> 7.91 us  [per_device(): gathered = lax.all_to_all(rows, ALL, 0, 0, tiled=True)]
    unnamed x11 -> x15, local copies, waits for them, and re-layouts: 0.76 us -> 3.67 us
    pallas_call x4 -> x5, Pallas kernels: 22.8 us -> 24.1 us  [stage(): return call(*operands)]
  transfers between devices with their start and end apart: 12 -> 14, of which waited for: 4 -> 3; matrix products, arithmetic and copies ran while one was open for 3% -> 3% of each run, Pallas kernels for 15% -> 15%
where the time goes in v1:
time: 141 us; the launch traced here: 140 us
  starting transfers between devices  57.1 us (40%)
  waiting for transfers between devices  44.9 us (32%)
  Pallas kernels  29.1 us (21%)
  local copies, waits for them, and re-layouts  7.79 us (6%)
    ppermute x13, starting transfers between devices, moved(): return lax.ppermute(array, ALL, route)  49.2 us
    ppermute x13, waiting for transfers between devices, moved(): return lax.ppermute(array, ALL, route)  35.5 us
    pallas_call x5, Pallas kernels, stage(): return call(*operands)  24.1 us
    all_to_all x1, waiting for transfers between devices, per_device(): gathered = lax.all_to_all(rows, ALL, 0, 0, tiled=True)  9.49 us
    all_to_all x1, starting transfers between devices, per_device(): gathered = lax.all_to_all(rows, ALL, 0, 0, tiled=True)  7.91 us
    unnamed x15, local copies, waits for them, and re-layouts  3.67 us
    pallas_call x2, Pallas kernels, per_device(): ready = mark(zero(table), own)  3.37 us
  transfers between devices with their start and end apart: 14, of which 3 were waited for; matrix products, arithmetic and copies ran while one was open for 3% of the time, Pallas kernels for 15%

profile of v1, /device:TPU:1, one launch (start us, length us, event | category | flops | bytes accessed | tf_op | source)
XLA Modules:
  0.0 140.1 jit_solution(18132605278891483341)
XLA Ops:
  0.7 0.9 collective-permute-start.3
  1.6 13.0 %collective-permute-start.5 = (bf16[2,2,512,512]{3,2,1,0:T(8,128)(2,1)}, bf16[2,2,512,512]{3,2,1,0:T(8,128)(2,1)}, u32[]{:S(2)}, u32[]{:S(2)}) collective-permute-start(bf16[2,2,512,512]{3,2,1,0:T(8,128)(2,1)} %bitcast.6), channel_id=1, source_target_pairs={{2,255},{3,254},{6,2},{7,3},{10,6},{11,7},{14,10},{15,11},{18,14},... | collective-permute-start | bytes 6291464 | tf_op jit(solution)/shard_map/ppermute | solution.py:81
  14.6 2.0 %collective-permute-start.11 = (bf16[2,2,512,512]{3,2,1,0:T(8,128)(2,1)}, bf16[2,2,512,512]{3,2,1,0:T(8,128)(2,1)}, u32[]{:S(2)}, u32[]{:S(2)}) collective-permute-start(bf16[2,2,512,512]{3,2,1,0:T(8,128)(2,1)} %bitcast.7), channel_id=1, source_target_pairs={{0,253},{1,252},{4,0},{5,1},{8,4},{9,5},{12,8},{13,9},{16,12},{17,... | collective-permute-start | bytes 6291464 | tf_op jit(solution)/shard_map/ppermute | solution.py:81
  16.6 2.0 %collective-permute-start.4 = (bf16[2,2,512,512]{3,2,1,0:T(8,128)(2,1)S(1)}, bf16[2,2,512,512]{3,2,1,0:T(8,128)(2,1)}, u32[]{:S(2)}, u32[]{:S(2)}) collective-permute-start(bf16[2,2,512,512]{3,2,1,0:T(8,128)(2,1)S(1)} %collective-permute-done.3), channel_id=1, source_target_pairs={{4,249},{5,248},{249,253},{248,252},{12,0},{13,1},{0,4},{1,5},{20,... | collective-permute-start | bytes 6291464 | tf_op jit(solution)/shard_map/ppermute | solution.py:81
  18.6 1.5 %collective-permute-start = (s32[3,2]{0,1:T(2,128)}, s32[3,2]{0,1:T(2,128)S(1)}, u32[]{:S(2)}, u32[]{:S(2)}) collective-permute-start(s32[3,2]{0,1:T(2,128)} %param.4), channel_id=1, source_target_pairs={{0,1},{1,0},{2,3},{3,2},{4,5},{5,4},{6,7},{7,6},{8,9},{9,8},{10,11... | collective-permute-start | bytes 80 | tf_op jit(solution)/shard_map/ppermute | solution.py:81
  20.0 1.0 slice.9
  21.0 23.0 %collective-permute-done = s32[3,2]{0,1:T(2,128)S(1)} collective-permute-done((s32[3,2]{0,1:T(2,128)}, s32[3,2]{0,1:T(2,128)S(1)}, u32[]{:S(2)}, u32[]{:S(2)}) %collective-permute-start) | collective-permute-done | bytes 56 | tf_op jit(solution)/shard_map/ppermute | solution.py:81
  44.1 1.9 %collective-permute-start.7 = (bf16[2,2,96,512]{3,2,1,0:T(8,128)(2,1)S(1)}, bf16[2,2,96,512]{3,2,1,0:T(8,128)(2,1)S(1)}, u32[]{:S(2)}, u32[]{:S(2)}) collective-permute-start(bf16[2,2,96,512]{3,2,1,0:T(8,128)(2,1)S(1)} %slice.9), channel_id=1, source_target_pairs={{2,6},{3,7},{6,251},{7,250},{10,14},{11,15},{14,2},{15,3},{18,22},... | collective-permute-start | bytes 1179656 | tf_op jit(solution)/shard_map/ppermute | solution.py:81
  46.0 12.4 %collective-permute-done.7 = bf16[2,2,96,512]{3,2,1,0:T(8,128)(2,1)S(1)} collective-permute-done((bf16[2,2,96,512]{3,2,1,0:T(8,128)(2,1)S(1)}, bf16[2,2,96,512]{3,2,1,0:T(8,128)(2,1)S(1)}, u32[]{:S(2)}, u32[]{:S(2)}) %collective-permute-start.7) | collective-permute-done | bytes 393248 | tf_op jit(solution)/shard_map/ppermute | solution.py:81
  58.4 12.6 %collective-permute-start.2 = (bf16[2,2,512,512]{3,2,1,0:T(8,128)(2,1)}, bf16[2,2,512,512]{3,2,1,0:T(8,128)(2,1)}, u32[]{:S(2)}, u32[]{:S(2)}) collective-permute-start(bf16[2,2,512,512]{3,2,1,0:T(8,128)(2,1)} %bitcast.10), channel_id=1, source_target_pairs={{2,0},{3,1},{6,4},{7,5},{10,8},{11,9},{14,12},{15,13},{18,16},{19,... | collective-permute-start | bytes 6291464 | tf_op jit(solution)/shard_map/ppermute | solution.py:81
  71.0 2.7 %collective-permute-start.10 = (bf16[2,2,512,512]{3,2,1,0:T(8,128)(2,1)}, bf16[2,2,512,512]{3,2,1,0:T(8,128)(2,1)}, u32[]{:S(2)}, u32[]{:S(2)}) collective-permute-start(bf16[2,2,512,512]{3,2,1,0:T(8,128)(2,1)} %collective-permute-done.5.later1), channel_id=1, source_target_pairs={{2,0},{3,1},{6,4},{7,5},{10,8},{11,9},{14,12},{15,13},{18,16},{19,... | collective-permute-start | bytes 6291464 | tf_op jit(solution)/shard_map/ppermute | solution.py:81
  73.7 1.3 collective-permute-start.12
  75.0 1.3 collective-permute-start.9
  76.3 2.8 %slice.8 = bf16[2,2,416,512]{3,2,1,0:T(8,128)(2,1)} slice(bf16[2,2,512,512]{3,2,1,0:T(8,128)(2,1)} %collective-permute-done.5.later1), slice={[0:2], [0:2], [0:416], [0:512]} | slice | bytes 3407872 | tf_op jit(solution)/shard_map/slice | solution.py:305
  79.1 1.3 copy-done.2
  80.4 5.5 %collective-permute-start.6 = (bf16[2,2,416,512]{3,2,1,0:T(8,128)(2,1)}, bf16[2,2,416,512]{3,2,1,0:T(8,128)(2,1)}, u32[]{:S(2)}, u32[]{:S(2)}) collective-permute-start(bf16[2,2,416,512]{3,2,1,0:T(8,128)(2,1)} %slice.8), channel_id=1, source_target_pairs={{2,255},{3,254},{6,2},{7,3},{10,6},{11,7},{14,10},{15,11},{18,14},... | collective-permute-start | bytes 5111816 | tf_op jit(solution)/shard_map/ppermute | solution.py:81
  85.9 0.1 copy.7
  86.0 0.1 reshape.10
  86.0 0.1 copy.8
  86.3 4.7 %collective-permute-start.8 = (bf16[2,2,96,512]{3,2,1,0:T(8,128)(2,1)S(1)}, bf16[2,2,96,512]{3,2,1,0:T(8,128)(2,1)S(1)}, u32[]{:S(2)}, u32[]{:S(2)}) collective-permute-start(bf16[2,2,96,512]{3,2,1,0:T(8,128)(2,1)S(1)} %collective-permute-done.7), channel_id=1, source_target_pairs={{6,251},{7,250},{251,255},{250,254},{14,2},{15,3},{2,6},{3,7},{22,... | collective-permute-start | bytes 1179656 | tf_op jit(solution)/shard_map/ppermute | solution.py:81
  91.0 1.6 %copy-done.3 = bf16[2,2,512,512]{3,2,1,0:T(8,128)(2,1)S(1)} copy-done((bf16[2,2,512,512]{3,2,1,0:T(8,128)(2,1)S(1)}, bf16[2,2,512,512]{3,2,1,0:T(8,128)(2,1)}, u32[]{:S(2)}) %copy-start.3) | copy-done | bytes 2097176
  92.6 0.6 shard_map.50
  93.2 5.9 %shard_map.51.before = f32[1,128]{1,0:T(1,128)S(1)} custom-call(s32[18]{0:T(128)S(1)} %concatenate.3.table_in.table, bf16[4,2,512,512]{3,2,1,0:T(8,128)(2,1)S(1)} %get-tuple-element.6.fields, bf16[2,2,512,512]{3,2,1,0:T(8,128)(2,1)} %collective-permute-done.11.later0, bf16[2,2,512,512]{3,2,1,0:T(8,128)(2,1)} %collective-permute-done.5.later1, ...), custom_call_target="tpu_custom_call" | custom-call | flops 3221225472 | bytes 5242880 | tf_op jit(solution)/shard_map/pallas_call | solution.py:225
  99.2 6.1 %shard_map.52.before = f32[1,128]{1,0:T(1,128)S(1)} custom-call(s32[18]{0:T(128)S(1)} %concatenate.3.table_in.table, bf16[4,2,512,512]{3,2,1,0:T(8,128)(2,1)S(1)} %get-tuple-element.6.fields, bf16[2,2,512,512]{3,2,1,0:T(8,128)(2,1)} %collective-permute-done.10.later0, bf16[2,2,512,512]{3,2,1,0:T(8,128)(2,1)} %collective-permute-done.12.later1, ...), custom_call_target="tpu_custom_call" | custom-call | flops 3221225472 | bytes 5242880 | tf_op jit(solution)/shard_map/pallas_call | solution.py:225
  105.3 5.3 %shard_map.53.before = f32[1,128]{1,0:T(1,128)S(1)} custom-call(s32[18]{0:T(128)S(1)} %concatenate.3.table_in.table, bf16[4,2,512,512]{3,2,1,0:T(8,128)(2,1)S(1)} %get-tuple-element.6.fields, bf16[2,2,512,512]{3,2,1,0:T(8,128)(2,1)} %collective-permute-done.9.later, f32[1,128]{1,0:T(1,128)S(1)} %shard_map.52.before), custom_call_target="tpu_custom_call" | custom-call | flops 3221225472 | bytes 5242880 | tf_op jit(solution)/shard_map/pallas_call | solution.py:225
  110.6 6.1 %shard_map.54 = f32[256,1,128]{2,1,0:T(1,128)} custom-call(s32[18]{0:T(128)S(1)} %concatenate.3.table_in.table, bf16[4,2,512,512]{3,2,1,0:T(8,128)(2,1)S(1)} %get-tuple-element.6.fields, bf16[2,2,512,512]{3,2,1,0:T(8,128)(2,1)} %collective-permute-done.4.around, bf16[2,2,416,512]{3,2,1,0:T(8,128)(2,1)} %collective-permute-done.6.onward, ...), custom_call_target="tpu_custom_call" | custom-call | flops 3221225472 | bytes 5242880 | tf_op jit(solution)/shard_map/pallas_call | solution.py:225
  116.8 7.9 %all-to-all-start = ((f32[256,1,128]{2,1,0:T(1,128)}), f32[256,1,128]{2,1,0:T(1,128)S(1)}, u32[]{:S(2)}, u32[]{:S(2)}) async-start(f32[256,1,128]{2,1,0:T(1,128)} %shard_map.54), calls=%async_computation | async-start | bytes 262144 | tf_op jit(solution)/shard_map/all_to_all | solution.py:345
  124.7 1.2 zero.1.before
  125.8 2.2 %mark.1._ = f32[1,128]{1,0:T(1,128)} custom-call(f32[1,128]{1,0:T(1,128)} %zero.1.before, bf16[2,2,512,512]{3,2,1,0:T(8,128)(2,1)} %bitcast.11), custom_call_target="tpu_custom_call" | custom-call | tf_op jit(solution)/shard_map/mark/pallas_call | solution.py:302
  128.0 9.5 %all-to-all-done.gathered = f32[256,1,128]{2,1,0:T(1,128)S(1)} async-done(((f32[256,1,128]{2,1,0:T(1,128)}), f32[256,1,128]{2,1,0:T(1,128)S(1)}, u32[]{:S(2)}, u32[]{:S(2)}) %all-to-all-start) | async-done | bytes 131104 | tf_op jit(solution)/shard_map/all_to_all | solution.py:345
  137.5 0.6 copy-done.4
  138.2 1.7 %finish.1 = (f32[1,3,2,4]{3,2,1,0:T(2,128)}, f32[3,2,4]{2,1,0:T(2,128)}) custom-call(s32[18]{0:T(128)} %copy-done.1, f32[256,1,128]{2,1,0:T(1,128)} %copy-done.4, f32[1,128]{1,0:T(1,128)} %mark.1._), custom_call_target="tpu_custom_call" | custom-call | tf_op jit(solution)/shard_map/finish/pallas_call | solution.py:281
  (25 shorter events, 0.2 us)
Async XLA Ops:
  0.6 85.2 %copy-start.5 = (s32[3,2]{0,1:T(2,128)S(1)}, s32[3,2]{0,1:T(2,128)}, u32[]{:S(2)}) copy-start(s32[3,2]{0,1:T(2,128)} %param.4) | copy-start | bytes 76
  0.6 85.6 %copy-start.6 = (s32[4]{0:T(128)S(1)}, s32[4]{0:T(128)}, u32[]{:S(2)}) copy-start(s32[4]{0:T(128)} %param.5) | copy-start | bytes 52
  0.6 90.3 %copy-start = (bf16[1,2,2,512,512]{4,3,2,1,0:T(8,128)(2,1)S(1)}, bf16[1,2,2,512,512]{4,3,2,1,0:T(8,128)(2,1)}, u32[]{:S(2)}) copy-start(bf16[1,2,2,512,512]{4,3,2,1,0:T(8,128)(2,1)} %param.3) | copy-start | bytes 6291460
  0.7 15.9 %collective-permute-start.3 = (bf16[2,2,512,512]{3,2,1,0:T(8,128)(2,1)}, bf16[2,2,512,512]{3,2,1,0:T(8,128)(2,1)S(1)}, u32[]{:S(2)}, u32[]{:S(2)}) collective-permute-start(bf16[2,2,512,512]{3,2,1,0:T(8,128)(2,1)} %bitcast.5), channel_id=1, source_target_pairs={{0,4},{1,5},{4,249},{5,248},{8,12},{9,13},{12,0},{13,1},{16,20},{1... | collective-permute-start | bytes 6291464 | tf_op jit(solution)/shard_map/ppermute | solution.py:81
  1.6 69.4 %collective-permute-start.5 = (bf16[2,2,512,512]{3,2,1,0:T(8,128)(2,1)}, bf16[2,2,512,512]{3,2,1,0:T(8,128)(2,1)}, u32[]{:S(2)}, u32[]{:S(2)}) collective-permute-start(bf16[2,2,512,512]{3,2,1,0:T(8,128)(2,1)} %bitcast.6), channel_id=1, source_target_pairs={{2,255},{3,254},{6,2},{7,3},{10,6},{11,7},{14,10},{15,11},{18,14},... | collective-permute-start | bytes 6291464 | tf_op jit(solution)/shard_map/ppermute | solution.py:81
  14.6 59.1 %collective-permute-start.11 = (bf16[2,2,512,512]{3,2,1,0:T(8,128)(2,1)}, bf16[2,2,512,512]{3,2,1,0:T(8,128)(2,1)}, u32[]{:S(2)}, u32[]{:S(2)}) collective-permute-start(bf16[2,2,512,512]{3,2,1,0:T(8,128)(2,1)} %bitcast.7), channel_id=1, source_target_pairs={{0,253},{1,252},{4,0},{5,1},{8,4},{9,5},{12,8},{13,9},{16,12},{17,... | collective-permute-start | bytes 6291464 | tf_op jit(solution)/shard_map/ppermute | solution.py:81
  16.6 58.4 %collective-permute-start.4 = (bf16[2,2,512,512]{3,2,1,0:T(8,128)(2,1)S(1)}, bf16[2,2,512,512]{3,2,1,0:T(8,128)(2,1)}, u32[]{:S(2)}, u32[]{:S(2)}) collective-permute-start(bf16[2,2,512,512]{3,2,1,0:T(8,128)(2,1)S(1)} %collective-permute-done.3), channel_id=1, source_target_pairs={{4,249},{5,248},{249,253},{248,252},{12,0},{13,1},{0,4},{1,5},{20,... | collective-permute-start | bytes 6291464 | tf_op jit(solution)/shard_map/ppermute | solution.py:81
  18.6 60.5 %collective-permute-start.1 = (bf16[2,2,512,512]{3,2,1,0:T(8,128)(2,1)}, bf16[2,2,512,512]{3,2,1,0:T(8,128)(2,1)S(1)}, u32[]{:S(2)}, u32[]{:S(2)}) collective-permute-start(bf16[2,2,512,512]{3,2,1,0:T(8,128)(2,1)} %bitcast.8), channel_id=1, source_target_pairs={{0,1},{1,0},{2,3},{3,2},{4,5},{5,4},{6,7},{7,6},{8,9},{9,8},{10,11... | collective-permute-start | bytes 6291464 | tf_op jit(solution)/shard_map/ppermute | solution.py:81
  18.6 25.5 %collective-permute-start = (s32[3,2]{0,1:T(2,128)}, s32[3,2]{0,1:T(2,128)S(1)}, u32[]{:S(2)}, u32[]{:S(2)}) collective-permute-start(s32[3,2]{0,1:T(2,128)} %param.4), channel_id=1, source_target_pairs={{0,1},{1,0},{2,3},{3,2},{4,5},{5,4},{6,7},{7,6},{8,9},{9,8},{10,11... | collective-permute-start | bytes 80 | tf_op jit(solution)/shard_map/ppermute | solution.py:81
  44.1 14.3 %collective-permute-start.7 = (bf16[2,2,96,512]{3,2,1,0:T(8,128)(2,1)S(1)}, bf16[2,2,96,512]{3,2,1,0:T(8,128)(2,1)S(1)}, u32[]{:S(2)}, u32[]{:S(2)}) collective-permute-start(bf16[2,2,96,512]{3,2,1,0:T(8,128)(2,1)S(1)} %slice.9), channel_id=1, source_target_pairs={{2,6},{3,7},{6,251},{7,250},{10,14},{11,15},{14,2},{15,3},{18,22},... | collective-permute-start | bytes 1179656 | tf_op jit(solution)/shard_map/ppermute | solution.py:81
  58.4 27.9 %collective-permute-start.2 = (bf16[2,2,512,512]{3,2,1,0:T(8,128)(2,1)}, bf16[2,2,512,512]{3,2,1,0:T(8,128)(2,1)}, u32[]{:S(2)}, u32[]{:S(2)}) collective-permute-start(bf16[2,2,512,512]{3,2,1,0:T(8,128)(2,1)} %bitcast.10), channel_id=1, source_target_pairs={{2,0},{3,1},{6,4},{7,5},{10,8},{11,9},{14,12},{15,13},{18,16},{19,... | collective-permute-start | bytes 6291464 | tf_op jit(solution)/shard_map/ppermute | solution.py:81
  71.0 28.1 %collective-permute-start.10 = (bf16[2,2,512,512]{3,2,1,0:T(8,128)(2,1)}, bf16[2,2,512,512]{3,2,1,0:T(8,128)(2,1)}, u32[]{:S(2)}, u32[]{:S(2)}) collective-permute-start(bf16[2,2,512,512]{3,2,1,0:T(8,128)(2,1)} %collective-permute-done.5.later1), channel_id=1, source_target_pairs={{2,0},{3,1},{6,4},{7,5},{10,8},{11,9},{14,12},{15,13},{18,16},{19,... | collective-permute-start | bytes 6291464 | tf_op jit(solution)/shard_map/ppermute | solution.py:81
  73.7 25.5 %collective-permute-start.12 = (bf16[2,2,512,512]{3,2,1,0:T(8,128)(2,1)}, bf16[2,2,512,512]{3,2,1,0:T(8,128)(2,1)}, u32[]{:S(2)}, u32[]{:S(2)}) collective-permute-start(bf16[2,2,512,512]{3,2,1,0:T(8,128)(2,1)} %collective-permute-done.11.later0), channel_id=1, source_target_pairs={{0,2},{1,3},{4,6},{5,7},{8,10},{9,11},{12,14},{13,15},{16,18},{17,... | collective-permute-start | bytes 6291464 | tf_op jit(solution)/shard_map/ppermute | solution.py:81
  75.0 30.3 %collective-permute-start.9 = (bf16[2,2,512,512]{3,2,1,0:T(8,128)(2,1)}, bf16[2,2,512,512]{3,2,1,0:T(8,128)(2,1)}, u32[]{:S(2)}, u32[]{:S(2)}) collective-permute-start(bf16[2,2,512,512]{3,2,1,0:T(8,128)(2,1)} %collective-permute-done.4.around), channel_id=1, source_target_pairs={{0,2},{1,3},{4,6},{5,7},{8,10},{9,11},{12,14},{13,15},{16,18},{17,... | collective-permute-start | bytes 6291464 | tf_op jit(solution)/shard_map/ppermute | solution.py:81
  79.1 1.3 copy-start.2
  80.4 30.2 %collective-permute-start.6 = (bf16[2,2,416,512]{3,2,1,0:T(8,128)(2,1)}, bf16[2,2,416,512]{3,2,1,0:T(8,128)(2,1)}, u32[]{:S(2)}, u32[]{:S(2)}) collective-permute-start(bf16[2,2,416,512]{3,2,1,0:T(8,128)(2,1)} %slice.8), channel_id=1, source_target_pairs={{2,255},{3,254},{6,2},{7,3},{10,6},{11,7},{14,10},{15,11},{18,14},... | collective-permute-start | bytes 5111816 | tf_op jit(solution)/shard_map/ppermute | solution.py:81
  86.3 24.3 %copy-start.1 = (s32[18]{0:T(128)}, s32[18]{0:T(128)S(1)}, u32[]{:S(2)}) copy-start(s32[18]{0:T(128)S(1)} %concatenate.3.table_in.table) | copy-start | bytes 220
  86.3 24.3 %collective-permute-start.8 = (bf16[2,2,96,512]{3,2,1,0:T(8,128)(2,1)S(1)}, bf16[2,2,96,512]{3,2,1,0:T(8,128)(2,1)S(1)}, u32[]{:S(2)}, u32[]{:S(2)}) collective-permute-start(bf16[2,2,96,512]{3,2,1,0:T(8,128)(2,1)S(1)} %collective-permute-done.7), channel_id=1, source_target_pairs={{6,251},{7,250},{251,255},{250,254},{14,2},{15,3},{2,6},{3,7},{22,... | collective-permute-start | bytes 1179656 | tf_op jit(solution)/shard_map/ppermute | solution.py:81
  91.0 1.6 %copy-start.3 = (bf16[2,2,512,512]{3,2,1,0:T(8,128)(2,1)S(1)}, bf16[2,2,512,512]{3,2,1,0:T(8,128)(2,1)}, u32[]{:S(2)}) copy-start(bf16[2,2,512,512]{3,2,1,0:T(8,128)(2,1)} %copy-done.2) | copy-start | bytes 6291460
  116.8 20.8 %all-to-all-start = ((f32[256,1,128]{2,1,0:T(1,128)}), f32[256,1,128]{2,1,0:T(1,128)S(1)}, u32[]{:S(2)}, u32[]{:S(2)}) async-start(f32[256,1,128]{2,1,0:T(1,128)} %shard_map.54), calls=%async_computation | async-start | bytes 262144 | tf_op jit(solution)/shard_map/all_to_all | solution.py:345
  137.5 0.7 copy-start.4

commit v2 on v1

--- a/solution.py
+++ b/solution.py
@@ -67,6 +67,10 @@
 
 def partner_group_route():
     return [(device(t, g), device(t, 1 - g)) for t, g in each()]
+
+
+def other_core_route():
+    return [(device(t, g), device(t ^ 1, g)) for t, g in each()]
 
 
 def to_core(core):
@@ -177,31 +181,21 @@
             )
 
 
-def late_body(table, fields, later, before, out, diff, total):
+def late_body(table, fields, around, late, before, out, diff, total):
     out[...] = before[...]
 
     @pl.when(table[TIME] % 2 == 1)
     def _():
-        out[...] = add_terms(table, fields, before[...], 3, [later], diff, total)
-
-
-def four_body(table, fields, around, onward, rest, before, out, around_in, diff, total, sems):
-    core = table[TIME] % 2
-
-    def put(*later):
-        result = add_terms(table, fields, before[...], 4, later, diff, total)
-        out[...] = jnp.broadcast_to(result[None], out.shape)
-
-    @pl.when(core == 0)
-    def _():
-        copy = pltpu.make_async_copy(around, around_in, sems.at[0])
-        copy.start()
-        copy.wait()
-        put(around_in)
-
-    @pl.when(core == 1)
-    def _():
-        put(onward, rest)
+        out[...] = add_terms(table, fields, before[...], 3, [late, around], diff, total)
+
+
+def four_body(table, fields, around, late, onward, rest, before, out, diff, total):
+    for core, pieces in enumerate(([around, late], [onward, rest])):
+
+        @pl.when(table[TIME] % 2 == core)
+        def _(pieces=pieces):
+            result = add_terms(table, fields, before[...], 4, pieces, diff, total)
+            out[...] = jnp.broadcast_to(result[None], out.shape)
 
 
 ROW = jax.ShapeDtypeStruct((1, 128), F32)
@@ -287,11 +281,13 @@
     time = lax.axis_index(TM).astype(jnp.int32)
     group = lax.axis_index("mom").astype(jnp.int32)
 
-    two1 = moved(own, of_core(ring_route(2), 1))
     other_pairs = moved(mom_pairs, partner_group_route())
     other = moved(own, partner_group_route())
-    around = moved(own, of_core(round_x_first(), 0))
-    near = moved(own, to_core(0))
+    two1 = moved(own, of_core(ring_route(2), 1))
+    near = moved(own, other_core_route())
+    half = N // 2
+    around = jnp.where(time % 2 == 0, own[:, :, :half], near[:, :, half:])
+    around = moved(around, round_x_first())
     table = jnp.concatenate(
         [jnp.stack([time, group]), mom_pairs.reshape(-1), other_pairs.reshape(-1), deltas]
     )
@@ -300,7 +296,7 @@
         mark_body, in_specs=[VMEM, VMEM], out_specs=VMEM, out_shape=ROW, name="mark"
     )
     ready = mark(zero(table), own)
-    around = moved(around, of_core(round_x_second(), 0))
+    around = moved(around, round_x_second())
     two0 = moved(own, of_core(ring_route(2), 0))
     onward = moved(two1[:, :, :ROWS], of_core(ring_route(2), 1))
     swap1 = moved(two1, to_core(0))
@@ -324,7 +320,7 @@
         WORK,
         3,
     )
-    late = moved(around, to_core(1))
+    late = moved(around, other_core_route())
     result = stage(
         functools.partial(by_core_body, seps=(3, 1)),
         (table, all_fields, swap1, swap0, result),
@@ -333,13 +329,15 @@
         WORK,
         3,
     )
-    result = stage(late_body, (table, all_fields, late, result), [SMEM] + [VMEM] * 3, ROW, WORK, 3)
+    result = stage(
+        late_body, (table, all_fields, around, late, result), [SMEM] + [VMEM] * 4, ROW, WORK, 3
+    )
     rows = stage(
         four_body,
-        (table, all_fields, around, onward, rest, result),
-        [SMEM, VMEM, ANYWHERE, VMEM, VMEM, VMEM],
+        (table, all_fields, around, late, onward, rest, result),
+        [SMEM] + [VMEM] * 6,
         jax.ShapeDtypeStruct((2 * TIMES, 1, 128), F32),
-        [PLANES] + WORK + [pltpu.SemaphoreType.DMA((1,))],
+        WORK,
         3,
     )
     gathered = lax.all_to_all(rows, ALL, 0, 0, tiled=True)

time: 141 us -> 151 us (1.071)
  waiting for transfers between devices: 44.9 us -> 73.2 us
  starting transfers between devices: 57.1 us -> 40.3 us
  local copies, waits for them, and re-layouts: 7.79 us -> 3.9 us
  other arithmetic: 0 us -> 1.65 us
    ppermute x13, waiting for transfers between devices: 35.5 us -> 63.7 us  [moved(): return lax.ppermute(array, ALL, route)]
    ppermute x13, starting transfers between devices: 49.2 us -> 33.3 us  [moved(): return lax.ppermute(array, ALL, route)]
    unnamed x15 -> x11, local copies, waits for them, and re-layouts: 3.67 us -> 0.76 us
    select_n x0 -> x1, other arithmetic: none -> 1.65 us  [per_device(): around = jnp.where(time % 2 == 0, own[:, :, :half], near[:, :, half:])]
  transfers between devices with their start and end apart: 14 -> 14, of which waited for: 3 -> 4; matrix products, arithmetic and copies ran while one was open for 3% -> 3% of each run, Pallas kernels for 15% -> 15%
where the time goes in v2:
time: 151 us; the launch traced here: 150 us
  waiting for transfers between devices  73.2 us (48%)
  starting transfers between devices  40.3 us (27%)
  Pallas kernels  30.3 us (20%)
  local copies, waits for them, and re-layouts  3.9 us (3%)
  other arithmetic  1.65 us (1%)
    ppermute x13, waiting for transfers between devices, moved(): return lax.ppermute(array, ALL, route)  63.7 us
    ppermute x13, starting transfers between devices, moved(): return lax.ppermute(array, ALL, route)  33.3 us
    pallas_call x5, Pallas kernels, stage(): return call(*operands)  25.2 us
    all_to_all x1, waiting for transfers between devices, per_device(): gathered = lax.all_to_all(rows, ALL, 0, 0, tiled=True)  9.5 us
    all_to_all x1, starting transfers between devices, per_device(): gathered = lax.all_to_all(rows, ALL, 0, 0, tiled=True)  7.07 us
    pallas_call x2, Pallas kernels, per_device(): ready = mark(zero(table), own)  3.36 us
  transfers between devices with their start and end apart: 14, of which 4 were waited for; matrix products, arithmetic and copies ran while one was open for 3% of the time, Pallas kernels for 15%

profile of v2, /device:TPU:1, one launch (start us, length us, event | category | flops | bytes accessed | tf_op | source)
XLA Modules:
  0.0 150.5 jit_solution(12457040930319898050)
XLA Ops:
  0.7 3.3 %collective-permute-start.2 = (bf16[2,2,512,512]{3,2,1,0:T(8,128)(2,1)}, bf16[2,2,512,512]{3,2,1,0:T(8,128)(2,1)}, u32[]{:S(2)}, u32[]{:S(2)}) collective-permute-start(bf16[2,2,512,512]{3,2,1,0:T(8,128)(2,1)} %bitcast.5), channel_id=1, source_target_pairs={{0,2},{1,3},{2,0},{3,1},{4,6},{5,7},{6,4},{7,5},{8,10},{9,11},{10,... | collective-permute-start | bytes 6291464 | tf_op jit(solution)/shard_map/ppermute | solution.py:85
  3.9 10.4 %collective-permute-start.6 = (bf16[2,2,512,512]{3,2,1,0:T(8,128)(2,1)}, bf16[2,2,512,512]{3,2,1,0:T(8,128)(2,1)}, u32[]{:S(2)}, u32[]{:S(2)}) collective-permute-start(bf16[2,2,512,512]{3,2,1,0:T(8,128)(2,1)} %bitcast.6), channel_id=1, source_target_pairs={{2,255},{3,254},{6,2},{7,3},{10,6},{11,7},{14,10},{15,11},{18,14},... | collective-permute-start | bytes 6291464 | tf_op jit(solution)/shard_map/ppermute | solution.py:85
  14.4 2.0 %collective-permute-start.11 = (bf16[2,2,512,512]{3,2,1,0:T(8,128)(2,1)}, bf16[2,2,512,512]{3,2,1,0:T(8,128)(2,1)}, u32[]{:S(2)}, u32[]{:S(2)}) collective-permute-start(bf16[2,2,512,512]{3,2,1,0:T(8,128)(2,1)} %bitcast.7), channel_id=1, source_target_pairs={{0,253},{1,252},{4,0},{5,1},{8,4},{9,5},{12,8},{13,9},{16,12},{17,... | collective-permute-start | bytes 6291464 | tf_op jit(solution)/shard_map/ppermute | solution.py:85
  16.3 1.7 %slice_select_fusion = bf16[2,2,256,512]{3,2,1,0:T(8,128)(2,1)S(1)} fusion(bf16[2,2,512,512]{3,2,1,0:T(8,128)(2,1)} %collective-permute-done.2.near, bf16[2,2,512,512]{3,2,1,0:T(8,128)(2,1)} %bitcast.8, pred[]{:T(512)S(6)} %eq.5), kind=kLoop, calls=%fused_computation | loop fusion | flops 524288 | bytes 3145729 | tf_op jit(solution)/shard_map/jit(_where)/select_n | solution.py:289
  18.0 0.1 collective-permute-start.3
  18.1 0.1 collective-permute-start.1
  18.2 39.3 %collective-permute-done.6.later1 = bf16[2,2,512,512]{3,2,1,0:T(8,128)(2,1)} collective-permute-done((bf16[2,2,512,512]{3,2,1,0:T(8,128)(2,1)}, bf16[2,2,512,512]{3,2,1,0:T(8,128)(2,1)}, u32[]{:S(2)}, u32[]{:S(2)}) %collective-permute-start.6) | collective-permute-done | bytes 2097184 | tf_op jit(solution)/shard_map/ppermute | solution.py:85
  57.5 2.7 %collective-permute-start.10 = (bf16[2,2,512,512]{3,2,1,0:T(8,128)(2,1)}, bf16[2,2,512,512]{3,2,1,0:T(8,128)(2,1)}, u32[]{:S(2)}, u32[]{:S(2)}) collective-permute-start(bf16[2,2,512,512]{3,2,1,0:T(8,128)(2,1)} %collective-permute-done.6.later1), channel_id=1, source_target_pairs={{2,0},{3,1},{6,4},{7,5},{10,8},{11,9},{14,12},{15,13},{18,16},{19,... | collective-permute-start | bytes 6291464 | tf_op jit(solution)/shard_map/ppermute | solution.py:85
  60.2 1.3 collective-permute-start.12
  61.6 0.1 collective-permute-start
  61.7 3.3 %collective-permute-done = s32[3,2]{0,1:T(2,128)S(1)} collective-permute-done((s32[3,2]{0,1:T(2,128)S(1)}, s32[3,2]{0,1:T(2,128)S(1)}, u32[]{:S(2)}, u32[]{:S(2)}) %collective-permute-start) | collective-permute-done | bytes 56 | tf_op jit(solution)/shard_map/ppermute | solution.py:85
  65.0 3.0 %collective-permute-start.8 = (bf16[2,2,96,512]{3,2,1,0:T(8,128)(2,1)S(1)}, bf16[2,2,96,512]{3,2,1,0:T(8,128)(2,1)S(1)}, u32[]{:S(2)}, u32[]{:S(2)}) collective-permute-start(bf16[2,2,96,512]{3,2,1,0:T(8,128)(2,1)S(1)} %slice.19), channel_id=1, source_target_pairs={{2,6},{3,7},{6,251},{7,250},{10,14},{11,15},{14,2},{15,3},{18,22},... | collective-permute-start | bytes 1179656 | tf_op jit(solution)/shard_map/ppermute | solution.py:85
  68.0 2.8 %slice.18 = bf16[2,2,416,512]{3,2,1,0:T(8,128)(2,1)} slice(bf16[2,2,512,512]{3,2,1,0:T(8,128)(2,1)} %collective-permute-done.6.later1), slice={[0:2], [0:2], [0:416], [0:512]} | slice | bytes 3407872 | tf_op jit(solution)/shard_map/slice | solution.py:301
  70.8 21.1 %collective-permute-done.8 = bf16[2,2,96,512]{3,2,1,0:T(8,128)(2,1)S(1)} collective-permute-done((bf16[2,2,96,512]{3,2,1,0:T(8,128)(2,1)S(1)}, bf16[2,2,96,512]{3,2,1,0:T(8,128)(2,1)S(1)}, u32[]{:S(2)}, u32[]{:S(2)}) %collective-permute-start.8) | collective-permute-done | bytes 393248 | tf_op jit(solution)/shard_map/ppermute | solution.py:85
  91.8 8.3 %collective-permute-start.7 = (bf16[2,2,416,512]{3,2,1,0:T(8,128)(2,1)}, bf16[2,2,416,512]{3,2,1,0:T(8,128)(2,1)}, u32[]{:S(2)}, u32[]{:S(2)}) collective-permute-start(bf16[2,2,416,512]{3,2,1,0:T(8,128)(2,1)} %slice.18), channel_id=1, source_target_pairs={{2,255},{3,254},{6,2},{7,3},{10,6},{11,7},{14,10},{15,11},{18,14},... | collective-permute-start | bytes 5111816 | tf_op jit(solution)/shard_map/ppermute | solution.py:85
  100.2 0.1 collective-permute-start.5
  100.3 0.1 copy.7
  100.4 0.1 reshape.10
  100.5 0.1 copy.8
  100.5 0.1 reshape.11
  100.7 1.9 %collective-permute-start.9 = (bf16[2,2,96,512]{3,2,1,0:T(8,128)(2,1)S(1)}, bf16[2,2,96,512]{3,2,1,0:T(8,128)(2,1)S(1)}, u32[]{:S(2)}, u32[]{:S(2)}) collective-permute-start(bf16[2,2,96,512]{3,2,1,0:T(8,128)(2,1)S(1)} %collective-permute-done.8), channel_id=1, source_target_pairs={{6,251},{7,250},{251,255},{250,254},{14,2},{15,3},{2,6},{3,7},{22,... | collective-permute-start | bytes 1179656 | tf_op jit(solution)/shard_map/ppermute | solution.py:85
  102.6 1.8 %shard_map.50 = (f32[1,128]{1,0:T(1,128)S(1)}, bf16[4,2,512,512]{3,2,1,0:T(8,128)(2,1)S(1)}) custom-call(s32[18]{0:T(128)S(1)} %concatenate.3.table_in.table, bf16[2,2,512,512]{3,2,1,0:T(8,128)(2,1)S(1)} %bitcast.12, bf16[2,2,512,512]{3,2,1,0:T(8,128)(2,1)} %collective-permute-done.1.other, bf16[2,2,512,512]{3,2,1,0:T(8,128)(2,1)} %collective-permute-done.2.near), custom_call_target="tpu_custom_call" | custom-call | flops 3221225472 | bytes 5242880 | tf_op jit(solution)/shard_map/pallas_call | solution.py:219
  104.4 6.1 %shard_map.51.before = f32[1,128]{1,0:T(1,128)S(1)} custom-call(s32[18]{0:T(128)S(1)} %concatenate.3.table_in.table, bf16[4,2,512,512]{3,2,1,0:T(8,128)(2,1)S(1)} %get-tuple-element.6.fields, bf16[2,2,512,512]{3,2,1,0:T(8,128)(2,1)} %collective-permute-done.11.later0, bf16[2,2,512,512]{3,2,1,0:T(8,128)(2,1)} %collective-permute-done.6.later1, ...), custom_call_target="tpu_custom_call" | custom-call | flops 3221225472 | bytes 5242880 | tf_op jit(solution)/shard_map/pallas_call | solution.py:219
  110.6 5.9 %shard_map.52.before = f32[1,128]{1,0:T(1,128)S(1)} custom-call(s32[18]{0:T(128)S(1)} %concatenate.3.table_in.table, bf16[4,2,512,512]{3,2,1,0:T(8,128)(2,1)S(1)} %get-tuple-element.6.fields, bf16[2,2,512,512]{3,2,1,0:T(8,128)(2,1)} %collective-permute-done.10.later0, bf16[2,2,512,512]{3,2,1,0:T(8,128)(2,1)} %collective-permute-done.12.later1, ...), custom_call_target="tpu_custom_call" | custom-call | flops 3221225472 | bytes 5242880 | tf_op jit(solution)/shard_map/pallas_call | solution.py:219
  116.5 5.2 %shard_map.53.before = f32[1,128]{1,0:T(1,128)S(1)} custom-call(s32[18]{0:T(128)S(1)} %concatenate.3.table_in.table, bf16[4,2,512,512]{3,2,1,0:T(8,128)(2,1)S(1)} %get-tuple-element.6.fields, bf16[2,2,256,512]{3,2,1,0:T(8,128)(2,1)S(1)} %collective-permute-done.4.around, bf16[2,2,256,512]{3,2,1,0:T(8,128)(2,1)} %collective-permute-done.5.late, ...), custom_call_target="tpu_custom_call" | custom-call | flops 3221225472 | bytes 5242880 | tf_op jit(solution)/shard_map/pallas_call | solution.py:219
  121.8 6.2 %shard_map.54 = f32[256,1,128]{2,1,0:T(1,128)} custom-call(s32[18]{0:T(128)S(1)} %concatenate.3.table_in.table, bf16[4,2,512,512]{3,2,1,0:T(8,128)(2,1)S(1)} %get-tuple-element.6.fields, bf16[2,2,256,512]{3,2,1,0:T(8,128)(2,1)S(1)} %collective-permute-done.4.around, bf16[2,2,256,512]{3,2,1,0:T(8,128)(2,1)} %collective-permute-done.5.late, ...), custom_call_target="tpu_custom_call" | custom-call | flops 3221225472 | bytes 5242880 | tf_op jit(solution)/shard_map/pallas_call | solution.py:219
  128.0 7.1 %all-to-all-start = ((f32[256,1,128]{2,1,0:T(1,128)}), f32[256,1,128]{2,1,0:T(1,128)S(1)}, u32[]{:S(2)}, u32[]{:S(2)}) async-start(f32[256,1,128]{2,1,0:T(1,128)} %shard_map.54), calls=%async_computation | async-start | bytes 262144 | tf_op jit(solution)/shard_map/all_to_all | solution.py:343
  135.0 1.2 zero.1.before
  136.2 2.2 %mark.1._ = f32[1,128]{1,0:T(1,128)} custom-call(f32[1,128]{1,0:T(1,128)} %zero.1.before, bf16[2,2,512,512]{3,2,1,0:T(8,128)(2,1)} %bitcast.9), custom_call_target="tpu_custom_call" | custom-call | tf_op jit(solution)/shard_map/mark/pallas_call | solution.py:298
  138.4 9.5 %all-to-all-done.gathered = f32[256,1,128]{2,1,0:T(1,128)S(1)} async-done(((f32[256,1,128]{2,1,0:T(1,128)}), f32[256,1,128]{2,1,0:T(1,128)S(1)}, u32[]{:S(2)}, u32[]{:S(2)}) %all-to-all-start) | async-done | bytes 131104 | tf_op jit(solution)/shard_map/all_to_all | solution.py:343
  147.9 0.6 copy-done.2
  148.6 1.7 %finish.1 = (f32[1,3,2,4]{3,2,1,0:T(2,128)}, f32[3,2,4]{2,1,0:T(2,128)}) custom-call(s32[18]{0:T(128)} %copy-done.1, f32[256,1,128]{2,1,0:T(1,128)} %copy-done.2, f32[1,128]{1,0:T(1,128)} %mark.1._), custom_call_target="tpu_custom_call" | custom-call | tf_op jit(solution)/shard_map/finish/pallas_call | solution.py:275
  (22 shorter events, 0.2 us)
Async XLA Ops:
  0.6 17.5 %copy-start = (bf16[1,2,2,512,512]{4,3,2,1,0:T(8,128)(2,1)S(1)}, bf16[1,2,2,512,512]{4,3,2,1,0:T(8,128)(2,1)}, u32[]{:S(2)}) copy-start(bf16[1,2,2,512,512]{4,3,2,1,0:T(8,128)(2,1)} %param.3) | copy-start | bytes 6291460
  0.6 60.9 %copy-start.3 = (s32[3,2]{0,1:T(2,128)S(1)}, s32[3,2]{0,1:T(2,128)}, u32[]{:S(2)}) copy-start(s32[3,2]{0,1:T(2,128)} %param.4) | copy-start | bytes 76
  0.7 15.7 %collective-permute-start.2 = (bf16[2,2,512,512]{3,2,1,0:T(8,128)(2,1)}, bf16[2,2,512,512]{3,2,1,0:T(8,128)(2,1)}, u32[]{:S(2)}, u32[]{:S(2)}) collective-permute-start(bf16[2,2,512,512]{3,2,1,0:T(8,128)(2,1)} %bitcast.5), channel_id=1, source_target_pairs={{0,2},{1,3},{2,0},{3,1},{4,6},{5,7},{6,4},{7,5},{8,10},{9,11},{10,... | collective-permute-start | bytes 6291464 | tf_op jit(solution)/shard_map/ppermute | solution.py:85
  3.9 53.6 %collective-permute-start.6 = (bf16[2,2,512,512]{3,2,1,0:T(8,128)(2,1)}, bf16[2,2,512,512]{3,2,1,0:T(8,128)(2,1)}, u32[]{:S(2)}, u32[]{:S(2)}) collective-permute-start(bf16[2,2,512,512]{3,2,1,0:T(8,128)(2,1)} %bitcast.6), channel_id=1, source_target_pairs={{2,255},{3,254},{6,2},{7,3},{10,6},{11,7},{14,10},{15,11},{18,14},... | collective-permute-start | bytes 6291464 | tf_op jit(solution)/shard_map/ppermute | solution.py:85
  14.4 45.8 %collective-permute-start.11 = (bf16[2,2,512,512]{3,2,1,0:T(8,128)(2,1)}, bf16[2,2,512,512]{3,2,1,0:T(8,128)(2,1)}, u32[]{:S(2)}, u32[]{:S(2)}) collective-permute-start(bf16[2,2,512,512]{3,2,1,0:T(8,128)(2,1)} %bitcast.7), channel_id=1, source_target_pairs={{0,253},{1,252},{4,0},{5,1},{8,4},{9,5},{12,8},{13,9},{16,12},{17,... | collective-permute-start | bytes 6291464 | tf_op jit(solution)/shard_map/ppermute | solution.py:85
  18.0 82.6 %copy-start.4 = (s32[4]{0:T(128)S(1)}, s32[4]{0:T(128)}, u32[]{:S(2)}) copy-start(s32[4]{0:T(128)} %param.5) | copy-start | bytes 52
  18.0 43.4 %collective-permute-start.3 = (bf16[2,2,256,512]{3,2,1,0:T(8,128)(2,1)S(1)}, bf16[2,2,256,512]{3,2,1,0:T(8,128)(2,1)S(1)}, u32[]{:S(2)}, u32[]{:S(2)}) collective-permute-start(bf16[2,2,256,512]{3,2,1,0:T(8,128)(2,1)S(1)} %slice_select_fusion), channel_id=1, source_target_pairs={{0,4},{1,5},{2,6},{3,7},{4,249},{5,248},{6,251},{7,250},{8,12},{9,... | collective-permute-start | bytes 3145736 | tf_op jit(solution)/shard_map/ppermute | solution.py:85
  18.1 82.6 %collective-permute-start.1 = (bf16[2,2,512,512]{3,2,1,0:T(8,128)(2,1)S(1)}, bf16[2,2,512,512]{3,2,1,0:T(8,128)(2,1)}, u32[]{:S(2)}, u32[]{:S(2)}) collective-permute-start(bf16[2,2,512,512]{3,2,1,0:T(8,128)(2,1)S(1)} %bitcast.10), channel_id=1, source_target_pairs={{0,1},{1,0},{2,3},{3,2},{4,5},{5,4},{6,7},{7,6},{8,9},{9,8},{10,11... | collective-permute-start | bytes 6291464 | tf_op jit(solution)/shard_map/ppermute | solution.py:85
  57.5 53.1 %collective-permute-start.10 = (bf16[2,2,512,512]{3,2,1,0:T(8,128)(2,1)}, bf16[2,2,512,512]{3,2,1,0:T(8,128)(2,1)}, u32[]{:S(2)}, u32[]{:S(2)}) collective-permute-start(bf16[2,2,512,512]{3,2,1,0:T(8,128)(2,1)} %collective-permute-done.6.later1), channel_id=1, source_target_pairs={{2,0},{3,1},{6,4},{7,5},{10,8},{11,9},{14,12},{15,13},{18,16},{19,... | collective-permute-start | bytes 6291464 | tf_op jit(solution)/shard_map/ppermute | solution.py:85
  60.2 50.4 %collective-permute-start.12 = (bf16[2,2,512,512]{3,2,1,0:T(8,128)(2,1)}, bf16[2,2,512,512]{3,2,1,0:T(8,128)(2,1)}, u32[]{:S(2)}, u32[]{:S(2)}) collective-permute-start(bf16[2,2,512,512]{3,2,1,0:T(8,128)(2,1)} %collective-permute-done.11.later0), channel_id=1, source_target_pairs={{0,2},{1,3},{4,6},{5,7},{8,10},{9,11},{12,14},{13,15},{16,18},{17,... | collective-permute-start | bytes 6291464 | tf_op jit(solution)/shard_map/ppermute | solution.py:85
  61.5 38.7 %collective-permute-start.4 = (bf16[2,2,256,512]{3,2,1,0:T(8,128)(2,1)S(1)}, bf16[2,2,256,512]{3,2,1,0:T(8,128)(2,1)S(1)}, u32[]{:S(2)}, u32[]{:S(2)}) collective-permute-start(bf16[2,2,256,512]{3,2,1,0:T(8,128)(2,1)S(1)} %collective-permute-done.3), channel_id=1, source_target_pairs={{4,249},{5,248},{6,251},{7,250},{249,253},{248,252},{251,255},{250... | collective-permute-start | bytes 3145736 | tf_op jit(solution)/shard_map/ppermute | solution.py:85
  61.6 3.5 %collective-permute-start = (s32[3,2]{0,1:T(2,128)S(1)}, s32[3,2]{0,1:T(2,128)S(1)}, u32[]{:S(2)}, u32[]{:S(2)}) collective-permute-start(s32[3,2]{0,1:T(2,128)S(1)} %copy-done.3), channel_id=1, source_target_pairs={{0,1},{1,0},{2,3},{3,2},{4,5},{5,4},{6,7},{7,6},{8,9},{9,8},{10,11... | collective-permute-start | bytes 80 | tf_op jit(solution)/shard_map/ppermute | solution.py:85
  65.0 26.8 %collective-permute-start.8 = (bf16[2,2,96,512]{3,2,1,0:T(8,128)(2,1)S(1)}, bf16[2,2,96,512]{3,2,1,0:T(8,128)(2,1)S(1)}, u32[]{:S(2)}, u32[]{:S(2)}) collective-permute-start(bf16[2,2,96,512]{3,2,1,0:T(8,128)(2,1)S(1)} %slice.19), channel_id=1, source_target_pairs={{2,6},{3,7},{6,251},{7,250},{10,14},{11,15},{14,2},{15,3},{18,22},... | collective-permute-start | bytes 1179656 | tf_op jit(solution)/shard_map/ppermute | solution.py:85
  91.8 29.9 %collective-permute-start.7 = (bf16[2,2,416,512]{3,2,1,0:T(8,128)(2,1)}, bf16[2,2,416,512]{3,2,1,0:T(8,128)(2,1)}, u32[]{:S(2)}, u32[]{:S(2)}) collective-permute-start(bf16[2,2,416,512]{3,2,1,0:T(8,128)(2,1)} %slice.18), channel_id=1, source_target_pairs={{2,255},{3,254},{6,2},{7,3},{10,6},{11,7},{14,10},{15,11},{18,14},... | collective-permute-start | bytes 5111816 | tf_op jit(solution)/shard_map/ppermute | solution.py:85
  100.2 16.4 %collective-permute-start.5 = (bf16[2,2,256,512]{3,2,1,0:T(8,128)(2,1)S(1)}, bf16[2,2,256,512]{3,2,1,0:T(8,128)(2,1)}, u32[]{:S(2)}, u32[]{:S(2)}) collective-permute-start(bf16[2,2,256,512]{3,2,1,0:T(8,128)(2,1)S(1)} %collective-permute-done.4.around), channel_id=1, source_target_pairs={{0,2},{1,3},{2,0},{3,1},{4,6},{5,7},{6,4},{7,5},{8,10},{9,11},{10,... | collective-permute-start | bytes 3145736 | tf_op jit(solution)/shard_map/ppermute | solution.py:85
  100.7 21.0 %copy-start.1 = (s32[18]{0:T(128)}, s32[18]{0:T(128)S(1)}, u32[]{:S(2)}) copy-start(s32[18]{0:T(128)S(1)} %concatenate.3.table_in.table) | copy-start | bytes 220
  100.7 21.0 %collective-permute-start.9 = (bf16[2,2,96,512]{3,2,1,0:T(8,128)(2,1)S(1)}, bf16[2,2,96,512]{3,2,1,0:T(8,128)(2,1)S(1)}, u32[]{:S(2)}, u32[]{:S(2)}) collective-permute-start(bf16[2,2,96,512]{3,2,1,0:T(8,128)(2,1)S(1)} %collective-permute-done.8), channel_id=1, source_target_pairs={{6,251},{7,250},{251,255},{250,254},{14,2},{15,3},{2,6},{3,7},{22,... | collective-permute-start | bytes 1179656 | tf_op jit(solution)/shard_map/ppermute | solution.py:85
  128.0 19.9 %all-to-all-start = ((f32[256,1,128]{2,1,0:T(1,128)}), f32[256,1,128]{2,1,0:T(1,128)S(1)}, u32[]{:S(2)}, u32[]{:S(2)}) async-start(f32[256,1,128]{2,1,0:T(1,128)} %shard_map.54), calls=%async_computation | async-start | bytes 262144 | tf_op jit(solution)/shard_map/all_to_all | solution.py:343
  147.9 0.6 copy-start.2
